TPU v7x, 32 devices: a whole 2x2x4 slice. The times are simulated.
32 devices in a mesh: rep: 2 (over y), blk: 8 (over z, x), head: 2 (over core).
Axes of the slice: x: 2, y: 2, z: 4, core: 2. Of those that a mesh axis runs over, the one named last changes fastest.
Arguments:
- queries: bfloat16 [2, 512, 8192], P('rep', 'blk', 'head'), parts along dimension 0, may hold values from -200 to 200
- keys: bfloat16 [2, 512, 512], P('rep', 'blk', 'head'), parts along dimension 0, may hold values from -6 to 6
- values: bfloat16 [2, 512, 512], P('rep', 'blk', 'head'), parts along dimension 0, may hold values from -6 to 6
- prompt_length: int32 [2], P('rep'), parts along dimension 0, may hold values from 256 to 512
- span_order: int32 [32], P('rep'), parts along dimension 0, may hold values from 0 to 15, as said below
Outputs:
- attended: bfloat16 [2, 512, 8192], P('rep', 'blk', 'head'), parts along dimension 0
There are 2 independent parts, one for each index of `rep`. A program takes and returns all parts, laid end to end along the dimension named above; each array names one. Nothing has to cross between parts.
Inputs may be any that keep to these rules, and one draw needn't show every extreme that they name: `span_order`: each of the 16 span numbers stands in exactly one slot.
All inputs are finite; a program needn't handle non-finite values.
Results may differ from a plain program's by a relative error of at most 0.0065.
Values may be sent and summed in bfloat16 or wider, within the bound.
A program may use at most 64 MiB of HBM per device.

v0:
```python
import functools
import math

import jax
import jax.numpy as jnp
from jax import lax
from jax.experimental import pallas as pl
from jax.experimental.pallas import tpu as pltpu
from jax.sharding import PartitionSpec as P

HEAD_WIDTH = 128
NEG_FILL = -1e30
HEADS_PER_TILE = 2
KEY_CHUNK = 512
OUT_PARTS = 2
VMEM_LIMIT = 56 * 1024 * 1024
MESH = pl.DeviceIdType.MESH


def row_length(blocks):
    return max(d for d in range(1, math.isqrt(blocks) + 1) if blocks % d == 0)


def kernel(
    rows_z, cols_x, local_heads, group, spans, q_hbm, k_hbm, v_hbm, len_hbm, order_hbm, o_hbm,
    q_ref, o_ref, k_ref, v_ref, bias_ref, w_ref, len_ref, order_ref, q_sem, own_sem, small_sem, out_sem,
    col_send, col_recv, row_send, row_recv
):
    blocks = rows_z * cols_x
    rows = q_ref.shape[0]
    span = rows // spans
    keys = blocks * rows
    me = lax.axis_index("blk")
    own = pl.ds(me * rows, rows)
    q_copy = pltpu.make_async_copy(q_hbm.at[0], q_ref, q_sem)
    k_copy = pltpu.make_async_copy(k_hbm.at[0], k_ref.at[own], own_sem.at[0])
    v_copy = pltpu.make_async_copy(v_hbm.at[0], v_ref.at[own], own_sem.at[1])
    k_copy.start()
    v_copy.start()
    q_copy.start()
    len_copy = pltpu.make_async_copy(len_hbm, len_ref, small_sem.at[0])
    order_copy = pltpu.make_async_copy(order_hbm, order_ref, small_sem.at[1])
    len_copy.start()
    order_copy.start()

    z, x = lax.div(me, cols_x), lax.rem(me, cols_x)
    refs = (k_ref, v_ref)

    def block(row, col):
        return pl.ds((row * cols_x + col) * rows, rows)

    def wrapped(row):
        return lax.rem(row + rows_z, rows_z)

    def peer(e):
        return z * cols_x + lax.rem(x + e, cols_x)

    def copy(u, at, target, send, recv):
        return pltpu.make_async_remote_copy(
            src_ref=refs[u].at[at],
            dst_ref=refs[u].at[at],
            send_sem=send,
            recv_sem=recv,
            device_id={"blk": target},
            device_id_type=MESH,
        )

    def to_column(row, u):
        return copy(u, own, row * cols_x + x, col_send.at[row, u], col_recv.at[z, u])

    def from_column(row, u):
        return copy(u, block(row, x), row * cols_x + x, col_send.at[row, u], col_recv.at[row, u])

    def to_row(row, e, u):
        return copy(u, block(row, x), peer(e), row_send.at[row, e - 1, u], row_recv.at[row, e - 1, u])

    def from_row(row, e, u):
        col = lax.rem(x + cols_x - e, cols_x)
        return copy(u, block(row, col), peer(e), row_send.at[row, e - 1, u], row_recv.at[row, e - 1, u])

    def each_row(distances, visit):
        for d in distances:
            pl.when(z + d < rows_z)(lambda d=d: visit(z + d))
            pl.when(z >= d)(lambda d=d: visit(z - d))

    near = range(1, rows_z)
    send_order = tuple(reversed(near))
    barrier = pltpu.get_barrier_semaphore()

    def greet(target):
        pl.semaphore_signal(barrier, inc=1, device_id={"blk": target}, device_id_type=MESH)

    for d in near:
        greet(lax.rem(me + d * cols_x, blocks))
    for e in range(1, cols_x):
        greet(peer(e))
    pl.semaphore_wait(barrier, rows_z + cols_x - 2)

    for u, own_copy in enumerate((k_copy, v_copy)):
        own_copy.wait()
        each_row(send_order, lambda row, u=u: to_column(row, u).start())
        for e in range(1, cols_x):
            to_row(z, e, u).start()

    def relay(row, u):
        from_column(row, u).wait_recv()
        for e in range(1, cols_x):
            to_row(row, e, u).start()

    def gather_row(row, u):
        for e in range(1, cols_x):
            from_row(row, e, u).wait_recv()

    def drain():
        for u in range(2):
            for d in near:
                to_column(lax.rem(z + d, rows_z), u).wait_send()
            for row in range(rows_z):
                for e in range(1, cols_x):
                    to_row(row, e, u).wait_send()

    len_copy.wait()
    order_copy.wait()
    limit = len_ref[0]
    row = lax.broadcasted_iota(jnp.int32, (rows, 1), 0)
    row_pos = jnp.zeros((rows, 1), jnp.int32)
    for t in range(spans):
        row_pos = jnp.where(row // span == t, order_ref[me * spans + t] * span + row % span, row_pos)
    chunk = min(keys, KEY_CHUNK)
    chunks = keys // chunk
    lane = lax.broadcasted_iota(jnp.int32, (1, chunk), 1)

    def make_bias(c):
        key_pos = jnp.zeros((1, chunk), jnp.int32)
        for t in range(chunk // span):
            key_pos = jnp.where(
                lane // span == t, order_ref[c * (chunk // span) + t] * span + lane % span, key_pos
            )
        allowed = (key_pos <= row_pos) & (key_pos < limit)
        bias_ref[c] = jnp.where(allowed, 0.0, NEG_FILL)

    pl.loop(0, chunks)(make_bias)
    live = row_pos < limit
    q_copy.wait()

    for u in range(2):
        each_row(tuple(reversed(near)), lambda row, u=u: relay(row, u))
    for row in range(rows_z):
        gather_row(row, 0)

    def gather_values():
        for row in range(rows_z):
            gather_row(row, 1)

    scale = HEAD_WIDTH ** (-0.5) * math.log2(math.e)
    tile = HEADS_PER_TILE if group % HEADS_PER_TILE == 0 else 1
    height = tile * rows
    ones = jnp.ones((chunk, HEAD_WIDTH), jnp.bfloat16)

    def out_copy(h, p):
        wide = group * HEAD_WIDTH // OUT_PARTS
        at = pl.ds((h * OUT_PARTS + p) * wide, wide)
        return pltpu.make_async_copy(o_ref.at[:, at], o_hbm.at[0, :, at], out_sem.at[h, p])

    if chunks > 1:
        gather_values()

    for phase, h in [(p, h) for p in range(2 if chunks == 1 else 1) for h in range(local_heads)]:
        if phase == 1 and h == 0:
            gather_values()
        cols = slice(h * HEAD_WIDTH, (h + 1) * HEAD_WIDTH)

        def run_tile(i, h=h, cols=cols, phase=phase):
            first = h * group * HEAD_WIDTH + i * (tile * HEAD_WIDTH)

            def q_cols(t):
                return pl.ds(pl.multiple_of(first + t * HEAD_WIDTH, HEAD_WIDTH), HEAD_WIDTH)

            kept = pl.ds(pl.multiple_of((h * (group // tile) + i) * height, height), height)
            q = jnp.concatenate([q_ref[:, q_cols(t)] for t in range(tile)], axis=0)

            def score_of(c):
                at = pl.ds(pl.multiple_of(c * chunk, chunk), chunk)
                score = lax.dot_general(
                    q, k_ref[at, cols], (((1,), (1,)), ((), ())), preferred_element_type=jnp.float32
                )
                score = (score * scale).reshape(tile, rows, chunk) + bias_ref[c][None]
                return score.reshape(height, chunk)

            def value_of(c):
                at = pl.ds(pl.multiple_of(c * chunk, chunk), chunk)
                return jnp.concatenate([v_ref[at, cols], ones], axis=1)

            if chunks == 1 and phase == 0:
                score = score_of(0)
                top = jnp.max(score, axis=1, keepdims=True)
                w_ref[kept] = jnp.exp2(score - top).astype(jnp.bfloat16)
                return
            if chunks == 1:
                mixed = jnp.dot(w_ref[kept], value_of(0), preferred_element_type=jnp.float32)
            else:

                def step(c, state):
                    best, mixed = state
                    score, value = score_of(c), value_of(c)
                    top = jnp.maximum(best, jnp.max(score, axis=1, keepdims=True))
                    weight = jnp.exp2(score - top).astype(jnp.bfloat16)
                    fresh = jnp.dot(weight, value, preferred_element_type=jnp.float32)
                    return top, mixed * jnp.exp2(best - top) + fresh

                init = (
                    jnp.full((height, 1), NEG_FILL, jnp.float32),
                    jnp.zeros((height, 2 * HEAD_WIDTH), jnp.float32),
                )
                _, mixed = lax.fori_loop(0, chunks, step, init)
            out = mixed[:, :HEAD_WIDTH] / mixed[:, HEAD_WIDTH:]
            for t in range(tile):
                piece = jnp.where(live, out[t * rows : (t + 1) * rows], 0.0)
                o_ref[:, q_cols(t)] = piece.astype(o_ref.dtype)

        tiles = group // tile
        per_part = tiles // OUT_PARTS
        for p in range(OUT_PARTS):
            pl.loop(p * per_part, (p + 1) * per_part, unroll=True)(run_tile)
            if phase == 1 or chunks > 1:
                out_copy(h, p).start()

    drain()
    for h in range(local_heads):
        for p in range(OUT_PARTS):
            out_copy(h, p).wait()


def solution(mesh):
    blocks = mesh.shape["blk"]
    cols_x = row_length(blocks)
    rows_z = blocks // cols_x

    def shards(queries, keys, values, prompt_length, span_order):
        _, rows, width = queries.shape
        kv_width = keys.shape[2]
        local_heads = kv_width // HEAD_WIDTH
        group = width // kv_width
        total = blocks * rows
        chunk = min(total, KEY_CHUNK)
        anywhere = pl.BlockSpec(memory_space=pltpu.HBM)
        return pl.pallas_call(
            functools.partial(kernel, rows_z, cols_x, local_heads, group, span_order.shape[0] // blocks),
            out_shape=jax.ShapeDtypeStruct(queries.shape, queries.dtype),
            in_specs=[anywhere] * 5,
            out_specs=anywhere,
            scratch_shapes=[
                *[pltpu.VMEM((rows, width), queries.dtype)] * 2,
                pltpu.VMEM((total, kv_width), keys.dtype),
                pltpu.VMEM((total, kv_width), values.dtype),
                pltpu.VMEM((total // chunk, rows, chunk), jnp.float32),
                pltpu.VMEM((local_heads * group * rows if chunk == total else rows, chunk), jnp.bfloat16),
                pltpu.SMEM(prompt_length.shape, jnp.int32),
                pltpu.SMEM(span_order.shape, jnp.int32),
                pltpu.SemaphoreType.DMA,
                pltpu.SemaphoreType.DMA((2,)),
                pltpu.SemaphoreType.DMA((2,)),
                pltpu.SemaphoreType.DMA((local_heads, OUT_PARTS)),
                *[pltpu.SemaphoreType.DMA((rows_z, 2))] * 2,
                *[pltpu.SemaphoreType.DMA((rows_z, cols_x, 2))] * 2,
            ],
            compiler_params=pltpu.CompilerParams(
                collective_id=0, has_side_effects=True, vmem_limit_bytes=VMEM_LIMIT
            ),
        )(queries, keys, values, prompt_length, span_order)

    spec = P("rep", "blk", "head")
    return jax.shard_map(
        shards, mesh=mesh, in_specs=(spec, spec, spec, P("rep"), P("rep")), out_specs=spec, check_vma=False
    )
```

profile of v0, /device:TPU:0, one launch (start us, length us, event | category | flops | bytes accessed | tf_op | source)
XLA Modules:
  0.0 19.5 jit_solution(4242067515717406178)
XLA Ops:
  0.7 17.0 %shard_map.55 = bf16[1,64,4096]{2,1,0:T(8,128)(2,1)} custom-call(bf16[1,64,4096]{2,1,0:T(8,128)(2,1)} %q_hbm.1, bf16[1,64,256]{2,1,0:T(8,128)(2,1)} %k_hbm.1, bf16[1,64,256]{2,1,0:T(8,128)(2,1)} %v_hbm.1, s32[1]{0:T(128)S(6)} %copy.7.len_hbm, s32[16]{0:T(128)} %order_hbm.1), custom_call_target="tpu_custom_call" | custom-call | tf_op jit(solution)/shard_map/pallas_call | solution.py:247
  17.7 1.9 %copy.8 = bf16[1,64,4096]{2,1,0:T(8,128)(2,1)} copy(bf16[1,64,4096]{2,1,0:T(8,128)(2,1)} %shard_map.55) | data formatting | bytes 1048576
where the time goes:
time: 19.7 us; the launch traced here: 19.5 us
  Pallas kernels  17 us (86%)
  local copies, waits for them, and re-layouts  1.87 us (9%)
  between operations  0.66 us (3%)
    pallas_call x1, Pallas kernels, shards(): pl.pallas_call(functools.partial(kernel, rows_z, cols_x, local_heads, gro...  17 us
    unnamed x1, local copies, waits for them, and re-layouts  1.87 us

commit v1 on v0

v1 whole, which is shorter than its diff:
```python
import functools
import math

import jax
import jax.numpy as jnp
from jax import lax
from jax.experimental import pallas as pl
from jax.experimental.pallas import tpu as pltpu
from jax.sharding import PartitionSpec as P

HEAD_WIDTH = 128
NEG_FILL = -1e30
HEADS_PER_TILE = 2
KEY_CHUNK = 512
OUT_PARTS = 2
VMEM_LIMIT = 40 * 1024 * 1024
MESH = pl.DeviceIdType.MESH


def row_length(blocks):
    return max(d for d in range(1, math.isqrt(blocks) + 1) if blocks % d == 0)


def positions(order_ref, first, spans, span, shape, axis):
    index = lax.broadcasted_iota(jnp.int32, shape, axis)
    position = jnp.zeros(shape, jnp.int32)
    for t in range(spans):
        position = jnp.where(index // span == t, order_ref[first + t] * span + index % span, position)
    return position


def fill_bias(bias_ref, order_ref, limit, row_pos, span):
    chunks, _, chunk = bias_ref.shape
    spans = chunk // span

    def make(c):
        key_pos = positions(order_ref, c * spans, spans, span, (1, chunk), 1)
        bias_ref[c] = jnp.where((key_pos <= row_pos) & (key_pos < limit), 0.0, NEG_FILL)

    pl.loop(0, chunks)(make)


def exchange(rows_z, cols_x, refs, loads, ready_z, ready_x, z_send, x_send, recv):
    blocks = rows_z * cols_x
    rows = refs[0].shape[0] // blocks
    me = lax.axis_index("blk")
    z, x = lax.div(me, cols_x), lax.rem(me, cols_x)

    def copy(u, row, col, to_row, to_col, send):
        at = pl.ds((row * cols_x + col) * rows, rows)
        return pltpu.make_async_remote_copy(
            src_ref=refs[u].at[at],
            dst_ref=refs[u].at[at],
            send_sem=send,
            recv_sem=recv.at[row, col, u],
            device_id={"blk": to_row * cols_x + to_col},
            device_id_type=MESH,
        )

    def z_copy(row, u):
        return copy(u, z, x, row, x, z_send.at[row, u])

    def x_copy(row, col, u):
        return copy(u, row, x, z, col, x_send.at[row, col, u])

    def above(d, visit):
        pl.when(z + d < rows_z)(lambda: visit(z + d))

    def below(d, visit):
        pl.when(z >= d)(lambda: visit(z - d))

    def right(visit):
        for e in range(1, cols_x):
            pl.when(x + e < cols_x)(lambda e=e: visit(x + e))

    def left(visit):
        for e in range(1, cols_x):
            pl.when(x >= e)(lambda e=e: visit(x - e))

    far = range(rows_z - 1, 0, -1)
    near = range(1, rows_z)
    barrier = pltpu.get_barrier_semaphore()

    def signal(sem, row, col):
        pl.semaphore_signal(sem, inc=1, device_id={"blk": row * cols_x + col}, device_id_type=MESH)

    for d in near:
        above(d, lambda row: signal(barrier, row, x))
    right(lambda col: signal(barrier, z, col))
    pl.when(z + x > 0)(lambda: pl.semaphore_wait(barrier, z + x))
    for d in far:
        below(d, lambda row: signal(ready_z.at[z], row, x))
    left(lambda col: signal(ready_x.at[x], z, col))

    for u in range(2):
        loads[u].wait()
        for d in far:
            below(d, lambda row: z_copy(row, u).start())
        left(lambda col: x_copy(z, col, u).start())

    def send_right(col):
        pl.semaphore_wait(ready_x.at[col], 1)
        for u in range(2):
            x_copy(z, col, u).start()

    def send_above(row):
        pl.semaphore_wait(ready_z.at[row], 1)
        for u in range(2):
            z_copy(row, u).start()

    right(send_right)
    for d in near:
        above(d, send_above)

    def relay(row, u):
        copy(u, row, x, z, x, z_send.at[row, u]).wait_recv()
        right(lambda col: x_copy(row, col, u).start())
        left(lambda col: x_copy(row, col, u).start())

    for u in range(2):
        for d in near:
            below(d, lambda row: relay(row, u))
            above(d, lambda row: relay(row, u))

    def arrived(u):
        for row in range(rows_z):
            def take(col, row=row):
                copy(u, row, col, z, x, x_send.at[row, x, u]).wait_recv()

            left(take)
            right(take)

    def drain():
        for u in range(2):
            for d in near:
                above(d, lambda row: z_copy(row, u).wait_send())
                below(d, lambda row: z_copy(row, u).wait_send())
            for row in range(rows_z):
                right(lambda col, row=row: x_copy(row, col, u).wait_send())
                left(lambda col, row=row: x_copy(row, col, u).wait_send())

    return arrived, drain


def own_loads(blocks, k_hbm, v_hbm, k_ref, v_ref, sem):
    rows = k_ref.shape[0] // blocks
    own = pl.ds(lax.axis_index("blk") * rows, rows)
    loads = [
        pltpu.make_async_copy(source.at[0], ref.at[own], sem.at[u])
        for u, (source, ref) in enumerate(((k_hbm, k_ref), (v_hbm, v_ref)))
    ]
    for load in loads:
        load.start()
    return loads


def gather_kernel(rows_z, cols_x, k_hbm, v_hbm, k_ref, v_ref, own_sem, *sems):
    loads = own_loads(rows_z * cols_x, k_hbm, v_hbm, k_ref, v_ref, own_sem)
    arrived, drain = exchange(rows_z, cols_x, (k_ref, v_ref), loads, *sems)
    arrived(0)
    arrived(1)
    drain()


def stacked_queries(q_ref, first, tile):
    def cols(t):
        return pl.ds(pl.multiple_of(first + t * HEAD_WIDTH, HEAD_WIDTH), HEAD_WIDTH)

    return cols, jnp.concatenate([q_ref[:, cols(t)] for t in range(tile)], axis=0)


def scores(q, keys, bias, tile):
    scale = HEAD_WIDTH ** (-0.5) * math.log2(math.e)
    score = lax.dot_general(q, keys, (((1,), (1,)), ((), ())), preferred_element_type=jnp.float32)
    rows, chunk = bias.shape
    return ((score * scale).reshape(tile, rows, chunk) + bias[None]).reshape(tile * rows, chunk)


def weight_kernel(
    rows_z, cols_x, group, spans, k_hbm, v_hbm, q_hbm, len_hbm, order_hbm, w_ref, v_ref, live_ref,
    q_ref, k_ref, bias_ref, len_ref, order_ref, q_sem, small_sem, own_sem, *sems
):
    loads = own_loads(rows_z * cols_x, k_hbm, v_hbm, k_ref, v_ref, own_sem)
    q_copy = pltpu.make_async_copy(q_hbm.at[0], q_ref, q_sem)
    len_copy = pltpu.make_async_copy(len_hbm, len_ref, small_sem.at[0])
    order_copy = pltpu.make_async_copy(order_hbm, order_ref, small_sem.at[1])
    len_copy.start()
    order_copy.start()
    q_copy.start()
    arrived, drain = exchange(rows_z, cols_x, (k_ref, v_ref), loads, *sems)

    rows = q_ref.shape[0]
    span = rows // spans
    len_copy.wait()
    order_copy.wait()
    limit = len_ref[0]
    row_pos = positions(order_ref, lax.axis_index("blk") * spans, spans, span, (rows, 1), 0)
    fill_bias(bias_ref, order_ref, limit, row_pos, span)
    live_ref[...] = jnp.broadcast_to(jnp.where(row_pos < limit, 1.0, 0.0), live_ref.shape)
    q_copy.wait()
    arrived(0)

    tile = HEADS_PER_TILE if group % HEADS_PER_TILE == 0 else 1
    height = tile * rows
    for h in range(k_ref.shape[1] // HEAD_WIDTH):
        cols = slice(h * HEAD_WIDTH, (h + 1) * HEAD_WIDTH)

        def weigh(i, h=h, cols=cols):
            _, q = stacked_queries(q_ref, (h * group + i * tile) * HEAD_WIDTH, tile)
            score = scores(q, k_ref[:, cols], bias_ref[0], tile)
            top = jnp.max(score, axis=1, keepdims=True)
            kept = pl.ds(pl.multiple_of((h * (group // tile) + i) * height, height), height)
            w_ref[kept] = jnp.exp2(score - top).astype(jnp.bfloat16)

        pl.loop(0, group // tile, unroll=True)(weigh)
    arrived(1)
    drain()


def store_heads(o_ref, mixed, live, cols, tile):
    rows = live.shape[0]
    out = mixed[:, :HEAD_WIDTH] / mixed[:, HEAD_WIDTH:]
    for t in range(tile):
        o_ref[:, cols(t)] = jnp.where(live, out[t * rows : (t + 1) * rows], 0.0).astype(o_ref.dtype)


def with_ones(values):
    return jnp.concatenate([values, jnp.ones((values.shape[0], HEAD_WIDTH), values.dtype)], axis=1)


def in_parts(o_hbm, o_ref, out_sem, local_heads, group, tile, visit):
    tiles = group // tile
    per_part = tiles // OUT_PARTS
    wide = group * HEAD_WIDTH // OUT_PARTS
    copies = []
    for h in range(local_heads):
        for p in range(OUT_PARTS):
            pl.loop(p * per_part, (p + 1) * per_part, unroll=True)(lambda i, h=h: visit(h, i))
            at = pl.ds((h * OUT_PARTS + p) * wide, wide)
            copies.append(pltpu.make_async_copy(o_ref.at[:, at], o_hbm.at[0, :, at], out_sem.at[h, p]))
            copies[-1].start()
    for copy in copies:
        copy.wait()


def mix_kernel(group, w_ref, v_ref, live_ref, o_hbm, o_ref, out_sem):
    tile = HEADS_PER_TILE if group % HEADS_PER_TILE == 0 else 1
    height = tile * live_ref.shape[0]
    live = live_ref[...] > 0.0

    def visit(h, i):
        first = (h * group + i * tile) * HEAD_WIDTH
        kept = pl.ds(pl.multiple_of((h * (group // tile) + i) * height, height), height)
        values = with_ones(v_ref[:, h * HEAD_WIDTH : (h + 1) * HEAD_WIDTH])
        mixed = jnp.dot(w_ref[kept], values, preferred_element_type=jnp.float32)

        def cols(t):
            return pl.ds(pl.multiple_of(first + t * HEAD_WIDTH, HEAD_WIDTH), HEAD_WIDTH)

        store_heads(o_ref, mixed, live, cols, tile)

    in_parts(o_hbm, o_ref, out_sem, v_ref.shape[1] // HEAD_WIDTH, group, tile, visit)


def attend_kernel(
    group, spans, q_hbm, k_ref, v_ref, len_hbm, order_hbm, o_hbm,
    q_ref, o_ref, bias_ref, len_ref, order_ref, q_sem, small_sem, out_sem
):
    q_copy = pltpu.make_async_copy(q_hbm.at[0], q_ref, q_sem)
    len_copy = pltpu.make_async_copy(len_hbm, len_ref, small_sem.at[0])
    order_copy = pltpu.make_async_copy(order_hbm, order_ref, small_sem.at[1])
    for copy in (len_copy, order_copy, q_copy):
        copy.start()
    rows = q_ref.shape[0]
    span = rows // spans
    len_copy.wait()
    order_copy.wait()
    limit = len_ref[0]
    row_pos = positions(order_ref, lax.axis_index("blk") * spans, spans, span, (rows, 1), 0)
    fill_bias(bias_ref, order_ref, limit, row_pos, span)
    live = row_pos < limit
    q_copy.wait()
    tile = HEADS_PER_TILE if group % HEADS_PER_TILE == 0 else 1
    height = tile * rows
    chunks, _, chunk = bias_ref.shape

    def visit(h, i):
        cols = slice(h * HEAD_WIDTH, (h + 1) * HEAD_WIDTH)
        q_cols, q = stacked_queries(q_ref, (h * group + i * tile) * HEAD_WIDTH, tile)

        def step(c, state):
            best, mixed = state
            at = pl.ds(pl.multiple_of(c * chunk, chunk), chunk)
            score = scores(q, k_ref[at, cols], bias_ref[c], tile)
            top = jnp.maximum(best, jnp.max(score, axis=1, keepdims=True))
            weight = jnp.exp2(score - top).astype(jnp.bfloat16)
            fresh = jnp.dot(weight, with_ones(v_ref[at, cols]), preferred_element_type=jnp.float32)
            return top, mixed * jnp.exp2(best - top) + fresh

        init = (
            jnp.full((height, 1), NEG_FILL, jnp.float32),
            jnp.zeros((height, 2 * HEAD_WIDTH), jnp.float32),
        )
        _, mixed = lax.fori_loop(0, chunks, step, init)
        store_heads(o_ref, mixed, live, q_cols, tile)

    in_parts(o_hbm, o_ref, out_sem, k_ref.shape[1] // HEAD_WIDTH, group, tile, visit)


def solution(mesh):
    blocks = mesh.shape["blk"]
    cols_x = row_length(blocks)
    rows_z = blocks // cols_x
    dma = pltpu.SemaphoreType.DMA
    hbm = pl.BlockSpec(memory_space=pltpu.HBM)
    vmem = pl.BlockSpec(memory_space=pltpu.VMEM)

    def shards(queries, keys, values, prompt_length, span_order):
        _, rows, width = queries.shape
        kv_width = keys.shape[2]
        local_heads = kv_width // HEAD_WIDTH
        group = width // kv_width
        total = blocks * rows
        chunk = min(total, KEY_CHUNK)
        spans = span_order.shape[0] // blocks
        queries, keys, values, span_order = (
            pltpu.with_memory_space_constraint(a, pltpu.HBM) for a in (queries, keys, values, span_order)
        )
        exchange_sems = [
            dma((2,)),
            pltpu.SemaphoreType.REGULAR((rows_z,)),
            pltpu.SemaphoreType.REGULAR((cols_x,)),
            dma((rows_z, 2)),
            dma((rows_z, cols_x, 2)),
            dma((rows_z, cols_x, 2)),
        ]
        small = [pltpu.SMEM(prompt_length.shape, jnp.int32), pltpu.SMEM(span_order.shape, jnp.int32)]
        talk = pltpu.CompilerParams(collective_id=0, has_side_effects=True, vmem_limit_bytes=VMEM_LIMIT)
        quiet = pltpu.CompilerParams(vmem_limit_bytes=VMEM_LIMIT)
        out_shape = jax.ShapeDtypeStruct(queries.shape, queries.dtype)
        out_sems = dma((local_heads, OUT_PARTS))
        gathered = pltpu.VMEM((total, kv_width), keys.dtype)
        bias = pltpu.VMEM((total // chunk, rows, chunk), jnp.float32)
        wide = pltpu.VMEM((rows, width), queries.dtype)
        if chunk == total:
            parts = pl.pallas_call(
                functools.partial(weight_kernel, rows_z, cols_x, group, spans),
                out_shape=[
                    pltpu.VMEM((local_heads * group * rows, total), jnp.bfloat16),
                    gathered,
                    pltpu.VMEM((rows, HEAD_WIDTH), jnp.float32),
                ],
                in_specs=[hbm] * 5,
                out_specs=[vmem] * 3,
                scratch_shapes=[wide, gathered, bias, *small, dma, dma((2,)), *exchange_sems],
                compiler_params=talk,
            )(keys, values, queries, prompt_length, span_order)
            return pl.pallas_call(
                functools.partial(mix_kernel, group),
                out_shape=out_shape,
                in_specs=[vmem] * 3,
                out_specs=hbm,
                scratch_shapes=[wide, out_sems],
                compiler_params=quiet,
            )(*parts)
        k_all, v_all = pl.pallas_call(
            functools.partial(gather_kernel, rows_z, cols_x),
            out_shape=[gathered] * 2,
            in_specs=[hbm] * 2,
            out_specs=[vmem] * 2,
            scratch_shapes=exchange_sems,
            compiler_params=talk,
        )(keys, values)
        return pl.pallas_call(
            functools.partial(attend_kernel, group, spans),
            out_shape=out_shape,
            in_specs=[hbm, vmem, vmem, hbm, hbm],
            out_specs=hbm,
            scratch_shapes=[wide, wide, bias, *small, dma, dma((2,)), out_sems],
            compiler_params=quiet,
        )(queries, k_all, v_all, prompt_length, span_order)

    spec = P("rep", "blk", "head")
    return jax.shard_map(
        shards, mesh=mesh, in_specs=(spec, spec, spec, P("rep"), P("rep")), out_specs=spec, check_vma=False
    )
```

time: 19.7 us -> 17.4 us (0.88)
  local copies, waits for them, and re-layouts: 1.87 us -> 0 us
  Pallas kernels: 17 us -> 16.6 us
    unnamed x1 -> x0, local copies, waits for them, and re-layouts: 1.87 us -> none
    pallas_call x1 -> x2, Pallas kernels: 17 us -> 16.6 us  [the longest x1 15.2 us: shards(): pl.pallas_call(functools.partial(weight_kernel, rows_z, cols_x, group, sp...]
where the time goes in v1:
time: 17.4 us; the launch traced here: 17.2 us
  Pallas kernels  16.6 us (95%)
  between operations  0.66 us (4%)
    pallas_call x1, Pallas kernels, shards(): pl.pallas_call(functools.partial(weight_kernel, rows_z, cols_x, group, sp...  15.2 us
    pallas_call x1, Pallas kernels, shards(): pl.pallas_call(functools.partial(mix_kernel, group), out_shape=out_shape,...  1.42 us

profile of v1, /device:TPU:0, one launch (start us, length us, event | category | flops | bytes accessed | tf_op | source)
XLA Modules:
  0.0 17.2 jit_solution(12807772191902420965)
XLA Ops:
  0.7 15.2 %shard_map.55 = (bf16[2048,512]{1,0:T(8,128)(2,1)S(1)}, bf16[512,256]{1,0:T(8,128)(2,1)S(1)}, f32[64,128]{1,0:T(8,128)S(1)}) custom-call(bf16[1,64,256]{2,1,0:T(8,128)(2,1)} %k_hbm.1, bf16[1,64,256]{2,1,0:T(8,128)(2,1)} %v_hbm.1, bf16[1,64,4096]{2,1,0:T(8,128)(2,1)} %q_hbm.1, s32[1]{0:T(128)S(6)} %copy.6.len_hbm, s32[16]{0:T(128)} %order_hbm.1), custom_call_target="tpu_custom_call" | custom-call | tf_op jit(solution)/shard_map/pallas_call | solution.py:346
  15.8 1.4 %shard_map.56 = bf16[1,64,4096]{2,1,0:T(8,128)(2,1)} custom-call(bf16[2048,512]{1,0:T(8,128)(2,1)S(1)} %get-tuple-element.8.w_ref, bf16[512,256]{1,0:T(8,128)(2,1)S(1)} %get-tuple-element.9.v_ref, f32[64,128]{1,0:T(8,128)S(1)} %get-tuple-element.10.live_ref), custom_call_target="tpu_custom_call" | custom-call | tf_op jit(solution)/shard_map/pallas_call | solution.py:358

commit v2 on v1

--- a/solution.py
+++ b/solution.py
@@ -29,39 +29,46 @@
     return position
 
 
-def fill_bias(bias_ref, order_ref, limit, row_pos, span):
+def fill_bias(bias_ref, order_ref, row_pos, span):
     chunks, _, chunk = bias_ref.shape
     spans = chunk // span
 
     def make(c):
         key_pos = positions(order_ref, c * spans, spans, span, (1, chunk), 1)
-        bias_ref[c] = jnp.where((key_pos <= row_pos) & (key_pos < limit), 0.0, NEG_FILL)
+        bias_ref[c] = jnp.where(key_pos <= row_pos, 0.0, NEG_FILL)
 
     pl.loop(0, chunks)(make)
 
 
-def exchange(rows_z, cols_x, refs, loads, ready_z, ready_x, z_send, x_send, recv):
-    blocks = rows_z * cols_x
-    rows = refs[0].shape[0] // blocks
+def exchange(rows_z, cols_x, sources, refs, meanwhile, own_sem, ready_z, ready_x, z_send, x_send, z_recv, x_recv):
+    rows = sources[0].shape[1]
     me = lax.axis_index("blk")
     z, x = lax.div(me, cols_x), lax.rem(me, cols_x)
-
-    def copy(u, row, col, to_row, to_col, send):
-        at = pl.ds((row * cols_x + col) * rows, rows)
+    even = lax.rem(z, 2) == 0
+    near = range(1, rows_z)
+    far = range(rows_z - 1, 0, -1)
+    own = pl.ds(me * rows, rows)
+    loads = [pltpu.make_async_copy(sources[u].at[0], refs[u].at[own], own_sem.at[u]) for u in range(2)]
+    for load in loads:
+        load.start()
+    meanwhile()
+
+    def send(source, u, row, to_row, to_col, send_sem, recv_sem):
+        at = pl.ds((row * cols_x + x) * rows, rows)
         return pltpu.make_async_remote_copy(
-            src_ref=refs[u].at[at],
+            src_ref=refs[u].at[at] if source is None else source,
             dst_ref=refs[u].at[at],
-            send_sem=send,
-            recv_sem=recv.at[row, col, u],
+            send_sem=send_sem,
+            recv_sem=recv_sem,
             device_id={"blk": to_row * cols_x + to_col},
             device_id_type=MESH,
         )
 
-    def z_copy(row, u):
-        return copy(u, z, x, row, x, z_send.at[row, u])
+    def z_copy(row, to_row, u, source=None):
+        return send(source, u, row, to_row, x, z_send.at[u], z_recv.at[row, u])
 
     def x_copy(row, col, u):
-        return copy(u, row, x, z, col, x_send.at[row, col, u])
+        return send(None, u, row, z, col, x_send.at[u], x_recv.at[u])
 
     def above(d, visit):
         pl.when(z + d < rows_z)(lambda: visit(z + d))
@@ -77,13 +84,14 @@
         for e in range(1, cols_x):
             pl.when(x >= e)(lambda e=e: visit(x - e))
 
-    far = range(rows_z - 1, 0, -1)
-    near = range(1, rows_z)
-    barrier = pltpu.get_barrier_semaphore()
+    def spread(row, u):
+        for e in range(1, cols_x):
+            x_copy(row, lax.rem(x + e, cols_x), u).start()
 
     def signal(sem, row, col):
         pl.semaphore_signal(sem, inc=1, device_id={"blk": row * cols_x + col}, device_id_type=MESH)
 
+    barrier = pltpu.get_barrier_semaphore()
     for d in near:
         above(d, lambda row: signal(barrier, row, x))
     right(lambda col: signal(barrier, z, col))
@@ -92,71 +100,135 @@
         below(d, lambda row: signal(ready_z.at[z], row, x))
     left(lambda col: signal(ready_x.at[x], z, col))
 
-    for u in range(2):
+    def direct(d, visit):
+        if d == 2:
+            pl.when(even)(visit)
+        else:
+            visit()
+
+    def send_below(u):
+        for d in far:
+            direct(d, lambda d=d: below(d, lambda row: z_copy(z, row, u, sources[u].at[0]).start()))
+
+    def send_above(d, *which):
+        def go(row):
+            for u in which:
+                z_copy(z, row, u, sources[u].at[0]).start()
+
+        if d != 3:
+            direct(d, lambda: above(d, go))
+
+    def answered(d):
+        above(d, lambda row: pl.semaphore_wait(ready_z.at[row], 1))
+
+    def relay_from_below(d, u):
+        def take(row):
+            z_copy(row, z, u).wait_recv()
+            if d == 1:
+                pl.when(even & (z + 1 < rows_z))(lambda: z_copy(row, z + 1, u).start())
+            if d == 2:
+                above(1, lambda to_row: z_copy(row, to_row, u).start())
+            spread(row, u)
+
+        below(d, take)
+
+    def relay_from_above(d, u):
+        def take(row):
+            z_copy(row, z, u).wait_recv()
+            spread(row, u)
+            if d == 1:
+                pl.when(even & (z >= 1))(lambda: z_copy(row, z - 1, u).start())
+
+        above(d, take)
+
+    def relay(d, u):
+        relay_from_below(d, u)
+        relay_from_above(d, u)
+
+    def send_left(u):
         loads[u].wait()
-        for d in far:
-            below(d, lambda row: z_copy(row, u).start())
         left(lambda col: x_copy(z, col, u).start())
 
-    def send_right(col):
-        pl.semaphore_wait(ready_x.at[col], 1)
+    def send_right(*which):
+        right(lambda col: pl.semaphore_wait(ready_x.at[col], 1))
+        for u in which:
+            right(lambda col: x_copy(z, col, u).start())
+
+    def eager():
         for u in range(2):
-            x_copy(z, col, u).start()
-
-    def send_above(row):
-        pl.semaphore_wait(ready_z.at[row], 1)
-        for u in range(2):
-            z_copy(row, u).start()
-
-    right(send_right)
-    for d in near:
-        above(d, send_above)
-
-    def relay(row, u):
-        copy(u, row, x, z, x, z_send.at[row, u]).wait_recv()
-        right(lambda col: x_copy(row, col, u).start())
-        left(lambda col: x_copy(row, col, u).start())
-
-    for u in range(2):
+            send_below(u)
+            send_left(u)
+        send_right(0, 1)
         for d in near:
-            below(d, lambda row: relay(row, u))
-            above(d, lambda row: relay(row, u))
+            answered(d)
+            send_above(d, 0, 1)
+
+        def lowest():
+            for u in range(2):
+                relay_from_above(1, u)
+            for u in range(2):
+                for d in near[1:]:
+                    relay_from_above(d, u)
+
+        def others():
+            for u in range(2):
+                for d in near:
+                    relay(d, u)
+
+        pl.when(z == 0)(lowest)
+        pl.when(z > 0)(others)
+
+    def patient():
+        send_below(0)
+        send_left(0)
+        right(lambda col: pl.semaphore_wait(ready_x.at[col], 1))
+        right(lambda col: x_copy(z, col, 0).start())
+        send_left(1)
+        right(lambda col: x_copy(z, col, 1).start())
+        for d in near:
+            answered(d)
+            send_above(d, 0)
+        for d in near:
+            relay(d, 0)
+            if d == 1:
+                send_below(1)
+                for further in near:
+                    send_above(further, 1)
+        for d in near:
+            relay(d, 1)
+
+    first = lax.axis_index("head") == 0
+    pl.when(first)(eager)
+    pl.when(~first)(patient)
+
+    def many(u, count, sem):
+        at = pl.ds(0, count * rows)
+        return pltpu.make_async_copy(refs[u].at[at], refs[u].at[at], sem)
+
+    along_x = (cols_x - 1) * rows_z
 
     def arrived(u):
-        for row in range(rows_z):
-            def take(col, row=row):
-                copy(u, row, col, z, x, x_send.at[row, x, u]).wait_recv()
-
-            left(take)
-            right(take)
+        many(u, along_x, x_recv.at[u]).wait()
+
+    def sent_along_z(row):
+        count = rows_z - 1 - (row + 3 < rows_z)
+        if row % 2 == 1:
+            count -= (row >= 2) + (row + 2 < rows_z)
+        elif 0 < row < rows_z - 1:
+            count += 2
+        return count + (row >= 2 and row + 1 < rows_z)
 
     def drain():
         for u in range(2):
-            for d in near:
-                above(d, lambda row: z_copy(row, u).wait_send())
-                below(d, lambda row: z_copy(row, u).wait_send())
+            many(u, along_x, x_send.at[u]).wait()
             for row in range(rows_z):
-                right(lambda col, row=row: x_copy(row, col, u).wait_send())
-                left(lambda col, row=row: x_copy(row, col, u).wait_send())
+                pl.when(z == row)(lambda row=row: many(u, sent_along_z(row), z_send.at[u]).wait())
 
     return arrived, drain
 
 
-def own_loads(blocks, k_hbm, v_hbm, k_ref, v_ref, sem):
-    rows = k_ref.shape[0] // blocks
-    own = pl.ds(lax.axis_index("blk") * rows, rows)
-    loads = [
-        pltpu.make_async_copy(source.at[0], ref.at[own], sem.at[u])
-        for u, (source, ref) in enumerate(((k_hbm, k_ref), (v_hbm, v_ref)))
-    ]
-    for load in loads:
-        load.start()
-    return loads
-
-
-def gather_kernel(rows_z, cols_x, k_hbm, v_hbm, k_ref, v_ref, own_sem, *sems):
-    loads = own_loads(rows_z * cols_x, k_hbm, v_hbm, k_ref, v_ref, own_sem)
-    arrived, drain = exchange(rows_z, cols_x, (k_ref, v_ref), loads, *sems)
+def gather_kernel(rows_z, cols_x, k_hbm, v_hbm, k_ref, v_ref, *sems):
+    arrived, drain = exchange(rows_z, cols_x, (k_hbm, v_hbm), (k_ref, v_ref), lambda: None, *sems)
     arrived(0)
     arrived(1)
     drain()
@@ -178,16 +250,15 @@
 
 def weight_kernel(
     rows_z, cols_x, group, spans, k_hbm, v_hbm, q_hbm, len_hbm, order_hbm, w_ref, v_ref, live_ref,
-    q_ref, k_ref, bias_ref, len_ref, order_ref, q_sem, small_sem, own_sem, *sems
+    q_ref, k_ref, bias_ref, len_ref, order_ref, q_sem, small_sem, *sems
 ):
-    loads = own_loads(rows_z * cols_x, k_hbm, v_hbm, k_ref, v_ref, own_sem)
     q_copy = pltpu.make_async_copy(q_hbm.at[0], q_ref, q_sem)
     len_copy = pltpu.make_async_copy(len_hbm, len_ref, small_sem.at[0])
     order_copy = pltpu.make_async_copy(order_hbm, order_ref, small_sem.at[1])
-    len_copy.start()
-    order_copy.start()
-    q_copy.start()
-    arrived, drain = exchange(rows_z, cols_x, (k_ref, v_ref), loads, *sems)
+    copies = (len_copy, order_copy, q_copy)
+    arrived, drain = exchange(
+        rows_z, cols_x, (k_hbm, v_hbm), (k_ref, v_ref), lambda: [copy.start() for copy in copies], *sems
+    )
 
     rows = q_ref.shape[0]
     span = rows // spans
@@ -195,7 +266,7 @@
     order_copy.wait()
     limit = len_ref[0]
     row_pos = positions(order_ref, lax.axis_index("blk") * spans, spans, span, (rows, 1), 0)
-    fill_bias(bias_ref, order_ref, limit, row_pos, span)
+    fill_bias(bias_ref, order_ref, row_pos, span)
     live_ref[...] = jnp.broadcast_to(jnp.where(row_pos < limit, 1.0, 0.0), live_ref.shape)
     q_copy.wait()
     arrived(0)
@@ -228,14 +299,14 @@
     return jnp.concatenate([values, jnp.ones((values.shape[0], HEAD_WIDTH), values.dtype)], axis=1)
 
 
-def in_parts(o_hbm, o_ref, out_sem, local_heads, group, tile, visit):
+def in_parts(o_hbm, o_ref, out_sem, local_heads, group, tile, visit, unroll):
     tiles = group // tile
     per_part = tiles // OUT_PARTS
     wide = group * HEAD_WIDTH // OUT_PARTS
     copies = []
     for h in range(local_heads):
         for p in range(OUT_PARTS):
-            pl.loop(p * per_part, (p + 1) * per_part, unroll=True)(lambda i, h=h: visit(h, i))
+            pl.loop(p * per_part, (p + 1) * per_part, unroll=unroll)(lambda i, h=h: visit(h, i))
             at = pl.ds((h * OUT_PARTS + p) * wide, wide)
             copies.append(pltpu.make_async_copy(o_ref.at[:, at], o_hbm.at[0, :, at], out_sem.at[h, p]))
             copies[-1].start()
@@ -259,7 +330,7 @@
 
         store_heads(o_ref, mixed, live, cols, tile)
 
-    in_parts(o_hbm, o_ref, out_sem, v_ref.shape[1] // HEAD_WIDTH, group, tile, visit)
+    in_parts(o_hbm, o_ref, out_sem, v_ref.shape[1] // HEAD_WIDTH, group, tile, visit, True)
 
 
 def attend_kernel(
@@ -277,7 +348,7 @@
     order_copy.wait()
     limit = len_ref[0]
     row_pos = positions(order_ref, lax.axis_index("blk") * spans, spans, span, (rows, 1), 0)
-    fill_bias(bias_ref, order_ref, limit, row_pos, span)
+    fill_bias(bias_ref, order_ref, row_pos, span)
     live = row_pos < limit
     q_copy.wait()
     tile = HEADS_PER_TILE if group % HEADS_PER_TILE == 0 else 1
@@ -304,7 +375,7 @@
         _, mixed = lax.fori_loop(0, chunks, step, init)
         store_heads(o_ref, mixed, live, q_cols, tile)
 
-    in_parts(o_hbm, o_ref, out_sem, k_ref.shape[1] // HEAD_WIDTH, group, tile, visit)
+    in_parts(o_hbm, o_ref, out_sem, k_ref.shape[1] // HEAD_WIDTH, group, tile, visit, False)
 
 
 def solution(mesh):
@@ -330,9 +401,10 @@
             dma((2,)),
             pltpu.SemaphoreType.REGULAR((rows_z,)),
             pltpu.SemaphoreType.REGULAR((cols_x,)),
+            dma((2,)),
+            dma((2,)),
             dma((rows_z, 2)),
-            dma((rows_z, cols_x, 2)),
-            dma((rows_z, cols_x, 2)),
+            dma((2,)),
         ]
         small = [pltpu.SMEM(prompt_length.shape, jnp.int32), pltpu.SMEM(span_order.shape, jnp.int32)]
         talk = pltpu.CompilerParams(collective_id=0, has_side_effects=True, vmem_limit_bytes=VMEM_LIMIT)

time: 17.4 us -> 15.5 us (0.89)
  the two profiles are of different devices: /device:TPU:0 before, /device:TPU:12 now
where the time goes in v2:
time: 15.5 us; the launch traced here: 15.4 us
  Pallas kernels  14.7 us (95%)
  between operations  0.66 us (4%)
    pallas_call x1, Pallas kernels, shards(): pl.pallas_call(functools.partial(weight_kernel, rows_z, cols_x, group, sp...  13.3 us
    pallas_call x1, Pallas kernels, shards(): pl.pallas_call(functools.partial(mix_kernel, group), out_shape=out_shape,...  1.42 us

profile of v2, /device:TPU:12, one launch (start us, length us, event | category | flops | bytes accessed | tf_op | source)
XLA Modules:
  0.0 15.4 jit_solution(2669402133592978121)
XLA Ops:
  0.7 13.3 %shard_map.55 = (bf16[2048,512]{1,0:T(8,128)(2,1)S(1)}, bf16[512,256]{1,0:T(8,128)(2,1)S(1)}, f32[64,128]{1,0:T(8,128)S(1)}) custom-call(bf16[1,64,256]{2,1,0:T(8,128)(2,1)} %k_hbm.1, bf16[1,64,256]{2,1,0:T(8,128)(2,1)} %v_hbm.1, bf16[1,64,4096]{2,1,0:T(8,128)(2,1)} %q_hbm.1, s32[1]{0:T(128)S(6)} %copy.6.len_hbm, s32[16]{0:T(128)} %order_hbm.1), custom_call_target="tpu_custom_call" | custom-call | tf_op jit(solution)/shard_map/pallas_call | solution.py:418
  13.9 1.4 %shard_map.56 = bf16[1,64,4096]{2,1,0:T(8,128)(2,1)} custom-call(bf16[2048,512]{1,0:T(8,128)(2,1)S(1)} %get-tuple-element.8.w_ref, bf16[512,256]{1,0:T(8,128)(2,1)S(1)} %get-tuple-element.9.v_ref, f32[64,128]{1,0:T(8,128)S(1)} %get-tuple-element.10.live_ref), custom_call_target="tpu_custom_call" | custom-call | tf_op jit(solution)/shard_map/pallas_call | solution.py:430

commit v3 on v2

--- a/solution.py
+++ b/solution.py
@@ -21,40 +21,47 @@
     return max(d for d in range(1, math.isqrt(blocks) + 1) if blocks % d == 0)
 
 
-def positions(order_ref, first, spans, span, shape, axis):
-    index = lax.broadcasted_iota(jnp.int32, shape, axis)
+def row_positions(order_ref, spans, rows):
+    span = rows // spans
+    index = lax.broadcasted_iota(jnp.int32, (rows, 1), 0)
+    position = jnp.zeros((rows, 1), jnp.int32)
+    for t in range(spans):
+        first = order_ref[lax.axis_index("blk") * spans + t] * span
+        position = jnp.where(index // span == t, first + index % span, position)
+    return position
+
+
+def key_positions(order_ref, first_block, shape, rows_z, cols_x, spans, rows):
+    span = rows // spans
+    index = lax.broadcasted_iota(jnp.int32, shape, 1)
     position = jnp.zeros(shape, jnp.int32)
-    for t in range(spans):
-        position = jnp.where(index // span == t, order_ref[first + t] * span + index % span, position)
+    for t in range(shape[1] // span):
+        slot = first_block + t // spans
+        block = lax.rem(slot, rows_z) * cols_x + lax.div(slot, rows_z)
+        first = order_ref[block * spans + t % spans] * span
+        position = jnp.where(index // span == t, first + index % span, position)
     return position
 
 
-def fill_bias(bias_ref, order_ref, row_pos, span):
-    chunks, _, chunk = bias_ref.shape
-    spans = chunk // span
-
-    def make(c):
-        key_pos = positions(order_ref, c * spans, spans, span, (1, chunk), 1)
-        bias_ref[c] = jnp.where(key_pos <= row_pos, 0.0, NEG_FILL)
-
-    pl.loop(0, chunks)(make)
-
-
-def exchange(rows_z, cols_x, sources, refs, meanwhile, own_sem, ready_z, ready_x, z_send, x_send, z_recv, x_recv):
+def mask(key_pos, row_pos):
+    return jnp.where(key_pos <= row_pos, 0.0, NEG_FILL)
+
+
+def exchange(rows_z, cols_x, sources, refs, meanwhile, prepare, own_keys, own_sem, ready_z, ready_x, z_send, x_send, z_recv, x_recv):
     rows = sources[0].shape[1]
     me = lax.axis_index("blk")
     z, x = lax.div(me, cols_x), lax.rem(me, cols_x)
     even = lax.rem(z, 2) == 0
     near = range(1, rows_z)
     far = range(rows_z - 1, 0, -1)
-    own = pl.ds(me * rows, rows)
+    own = pl.ds((x * rows_z + z) * rows, rows)
     loads = [pltpu.make_async_copy(sources[u].at[0], refs[u].at[own], own_sem.at[u]) for u in range(2)]
     for load in loads:
         load.start()
     meanwhile()
 
     def send(source, u, row, to_row, to_col, send_sem, recv_sem):
-        at = pl.ds((row * cols_x + x) * rows, rows)
+        at = pl.ds((x * rows_z + row) * rows, rows)
         return pltpu.make_async_remote_copy(
             src_ref=refs[u].at[at] if source is None else source,
             dst_ref=refs[u].at[at],
@@ -163,43 +170,38 @@
             answered(d)
             send_above(d, 0, 1)
 
-        def lowest():
-            for u in range(2):
-                relay_from_above(1, u)
-            for u in range(2):
-                for d in near[1:]:
-                    relay_from_above(d, u)
-
-        def others():
-            for u in range(2):
-                for d in near:
-                    relay(d, u)
-
-        pl.when(z == 0)(lowest)
-        pl.when(z > 0)(others)
-
     def patient():
         send_below(0)
         send_left(0)
-        right(lambda col: pl.semaphore_wait(ready_x.at[col], 1))
-        right(lambda col: x_copy(z, col, 0).start())
         send_left(1)
-        right(lambda col: x_copy(z, col, 1).start())
+        send_right(0, 1)
         for d in near:
             answered(d)
             send_above(d, 0)
-        for d in near:
-            relay(d, 0)
-            if d == 1:
-                send_below(1)
-                for further in near:
-                    send_above(further, 1)
-        for d in near:
-            relay(d, 1)
 
     first = lax.axis_index("head") == 0
     pl.when(first)(eager)
     pl.when(~first)(patient)
+    prepare()
+    lowest = first & (z == 0)
+
+    def values_now():
+        send_below(1)
+        for d in near:
+            send_above(d, 1)
+
+    for d in near:
+        relay(d, 0)
+        if d == 1:
+            pl.when(lowest)(lambda: relay_from_above(1, 1))
+            pl.when(~first)(values_now)
+    for d in near:
+        relay_from_below(d, 1)
+        if d == 1:
+            pl.when(~lowest)(lambda: relay_from_above(1, 1))
+        else:
+            relay_from_above(d, 1)
+    own_keys()
 
     def many(u, count, sem):
         at = pl.ds(0, count * rows)
@@ -228,7 +230,7 @@
 
 
 def gather_kernel(rows_z, cols_x, k_hbm, v_hbm, k_ref, v_ref, *sems):
-    arrived, drain = exchange(rows_z, cols_x, (k_hbm, v_hbm), (k_ref, v_ref), lambda: None, *sems)
+    arrived, drain = exchange(rows_z, cols_x, (k_hbm, v_hbm), (k_ref, v_ref), *[lambda: None] * 3, *sems)
     arrived(0)
     arrived(1)
     drain()
@@ -248,42 +250,72 @@
     return ((score * scale).reshape(tile, rows, chunk) + bias[None]).reshape(tile * rows, chunk)
 
 
-def weight_kernel(
-    rows_z, cols_x, group, spans, k_hbm, v_hbm, q_hbm, len_hbm, order_hbm, w_ref, v_ref, live_ref,
-    q_ref, k_ref, bias_ref, len_ref, order_ref, q_sem, small_sem, *sems
+def pair_kernel(
+    rows_z, cols_x, group, spans, k_hbm, v_hbm, q_hbm, len_hbm, order_hbm, w_ref, v_ref, acc_ref, live_ref,
+    q_ref, k_ref, own_w_ref, top_ref, bias_ref, len_ref, order_ref, q_sem, small_sem, *sems
 ):
+    rows = q_ref.shape[0]
+    half = rows_z * rows
+    x = lax.rem(lax.axis_index("blk"), cols_x)
+    own, other = (pl.ds(pl.multiple_of(side * half, half), half) for side in (x, 1 - x))
     q_copy = pltpu.make_async_copy(q_hbm.at[0], q_ref, q_sem)
     len_copy = pltpu.make_async_copy(len_hbm, len_ref, small_sem.at[0])
     order_copy = pltpu.make_async_copy(order_hbm, order_ref, small_sem.at[1])
     copies = (len_copy, order_copy, q_copy)
-    arrived, drain = exchange(
-        rows_z, cols_x, (k_hbm, v_hbm), (k_ref, v_ref), lambda: [copy.start() for copy in copies], *sems
-    )
-
-    rows = q_ref.shape[0]
-    span = rows // spans
-    len_copy.wait()
-    order_copy.wait()
-    limit = len_ref[0]
-    row_pos = positions(order_ref, lax.axis_index("blk") * spans, spans, span, (rows, 1), 0)
-    fill_bias(bias_ref, order_ref, row_pos, span)
-    live_ref[...] = jnp.broadcast_to(jnp.where(row_pos < limit, 1.0, 0.0), live_ref.shape)
-    q_copy.wait()
-    arrived(0)
-
     tile = HEADS_PER_TILE if group % HEADS_PER_TILE == 0 else 1
     height = tile * rows
-    for h in range(k_ref.shape[1] // HEAD_WIDTH):
-        cols = slice(h * HEAD_WIDTH, (h + 1) * HEAD_WIDTH)
-
-        def weigh(i, h=h, cols=cols):
-            _, q = stacked_queries(q_ref, (h * group + i * tile) * HEAD_WIDTH, tile)
-            score = scores(q, k_ref[:, cols], bias_ref[0], tile)
+    tiles = group // tile
+
+    def prepare():
+        for copy in copies:
+            copy.wait()
+        row_pos = row_positions(order_ref, spans, rows)
+        for n, side in enumerate((x, 1 - x)):
+            key_pos = key_positions(order_ref, side * rows_z, (1, half), rows_z, cols_x, spans, rows)
+            bias_ref[n] = mask(key_pos, row_pos)
+        live_ref[...] = jnp.broadcast_to(jnp.where(row_pos < len_ref[0], 1.0, 0.0), live_ref.shape)
+
+    def each_tile(visit):
+        for h in range(k_ref.shape[1] // HEAD_WIDTH):
+
+            def go(i, h=h):
+                kept = pl.ds(pl.multiple_of((h * tiles + i) * height, height), height)
+                visit(h * tiles + i, kept, slice(h * HEAD_WIDTH, (h + 1) * HEAD_WIDTH))
+
+            pl.loop(0, tiles, unroll=True)(go)
+
+    def own_keys():
+        def visit(n, kept, cols):
+            _, q = stacked_queries(q_ref, n * tile * HEAD_WIDTH, tile)
+            score = scores(q, k_ref[own, cols], bias_ref[0], tile)
             top = jnp.max(score, axis=1, keepdims=True)
-            kept = pl.ds(pl.multiple_of((h * (group // tile) + i) * height, height), height)
-            w_ref[kept] = jnp.exp2(score - top).astype(jnp.bfloat16)
-
-        pl.loop(0, group // tile, unroll=True)(weigh)
+            own_w_ref[kept] = jnp.exp2(score - top).astype(jnp.bfloat16)
+            top_ref[kept] = jnp.broadcast_to(top, (height, HEAD_WIDTH))
+
+        each_tile(visit)
+
+    arrived, drain = exchange(
+        rows_z, cols_x, (k_hbm, v_hbm), (k_ref, v_ref), lambda: [copy.start() for copy in copies], prepare, own_keys,
+        *sems
+    )
+
+    def own_values(n, kept, cols):
+        acc_ref[kept] = jnp.dot(own_w_ref[kept], with_ones(v_ref[own, cols]), preferred_element_type=jnp.float32)
+
+    each_tile(own_values)
+    arrived(0)
+
+    def other_keys(n, kept, cols):
+        _, q = stacked_queries(q_ref, n * tile * HEAD_WIDTH, tile)
+        score = scores(q, k_ref[other, cols], bias_ref[1], tile)
+        best = top_ref[kept]
+        top = jnp.maximum(best, jnp.max(score, axis=1, keepdims=True))
+        wide_top = jnp.concatenate([top] * (half // HEAD_WIDTH), axis=1)
+        w_ref[kept] = jnp.exp2(score - wide_top).astype(jnp.bfloat16)
+        fade = jnp.exp2(best - top)
+        acc_ref[kept] = acc_ref[kept] * jnp.concatenate([fade, fade], axis=1)
+
+    each_tile(other_keys)
     arrived(1)
     drain()
 
@@ -314,16 +346,19 @@
         copy.wait()
 
 
-def mix_kernel(group, w_ref, v_ref, live_ref, o_hbm, o_ref, out_sem):
+def mix_kernel(cols_x, group, w_ref, v_ref, acc_ref, live_ref, o_hbm, o_ref, out_sem):
     tile = HEADS_PER_TILE if group % HEADS_PER_TILE == 0 else 1
-    height = tile * live_ref.shape[0]
+    height = tile * o_ref.shape[0]
+    half = w_ref.shape[1]
+    side = 1 - lax.rem(lax.axis_index("blk"), cols_x)
+    other = pl.ds(pl.multiple_of(side * half, half), half)
     live = live_ref[...] > 0.0
 
     def visit(h, i):
         first = (h * group + i * tile) * HEAD_WIDTH
         kept = pl.ds(pl.multiple_of((h * (group // tile) + i) * height, height), height)
-        values = with_ones(v_ref[:, h * HEAD_WIDTH : (h + 1) * HEAD_WIDTH])
-        mixed = jnp.dot(w_ref[kept], values, preferred_element_type=jnp.float32)
+        values = with_ones(v_ref[other, h * HEAD_WIDTH : (h + 1) * HEAD_WIDTH])
+        mixed = acc_ref[kept] + jnp.dot(w_ref[kept], values, preferred_element_type=jnp.float32)
 
         def cols(t):
             return pl.ds(pl.multiple_of(first + t * HEAD_WIDTH, HEAD_WIDTH), HEAD_WIDTH)
@@ -334,7 +369,7 @@
 
 
 def attend_kernel(
-    group, spans, q_hbm, k_ref, v_ref, len_hbm, order_hbm, o_hbm,
+    rows_z, cols_x, group, spans, q_hbm, k_ref, v_ref, len_hbm, order_hbm, o_hbm,
     q_ref, o_ref, bias_ref, len_ref, order_ref, q_sem, small_sem, out_sem
 ):
     q_copy = pltpu.make_async_copy(q_hbm.at[0], q_ref, q_sem)
@@ -343,17 +378,20 @@
     for copy in (len_copy, order_copy, q_copy):
         copy.start()
     rows = q_ref.shape[0]
-    span = rows // spans
+    chunks, _, chunk = bias_ref.shape
     len_copy.wait()
     order_copy.wait()
-    limit = len_ref[0]
-    row_pos = positions(order_ref, lax.axis_index("blk") * spans, spans, span, (rows, 1), 0)
-    fill_bias(bias_ref, order_ref, row_pos, span)
-    live = row_pos < limit
+    row_pos = row_positions(order_ref, spans, rows)
+
+    def fill(c):
+        first = c * (chunk // rows)
+        bias_ref[c] = mask(key_positions(order_ref, first, (1, chunk), rows_z, cols_x, spans, rows), row_pos)
+
+    pl.loop(0, chunks)(fill)
+    live = row_pos < len_ref[0]
     q_copy.wait()
     tile = HEADS_PER_TILE if group % HEADS_PER_TILE == 0 else 1
     height = tile * rows
-    chunks, _, chunk = bias_ref.shape
 
     def visit(h, i):
         cols = slice(h * HEAD_WIDTH, (h + 1) * HEAD_WIDTH)
@@ -414,23 +452,36 @@
         gathered = pltpu.VMEM((total, kv_width), keys.dtype)
         bias = pltpu.VMEM((total // chunk, rows, chunk), jnp.float32)
         wide = pltpu.VMEM((rows, width), queries.dtype)
-        if chunk == total:
+        if chunk == total and cols_x == 2:
+            queue = local_heads * group * rows
+            half = total // 2
             parts = pl.pallas_call(
-                functools.partial(weight_kernel, rows_z, cols_x, group, spans),
+                functools.partial(pair_kernel, rows_z, cols_x, group, spans),
                 out_shape=[
-                    pltpu.VMEM((local_heads * group * rows, total), jnp.bfloat16),
+                    pltpu.VMEM((queue, half), jnp.bfloat16),
                     gathered,
+                    pltpu.VMEM((queue, 2 * HEAD_WIDTH), jnp.float32),
                     pltpu.VMEM((rows, HEAD_WIDTH), jnp.float32),
                 ],
                 in_specs=[hbm] * 5,
-                out_specs=[vmem] * 3,
-                scratch_shapes=[wide, gathered, bias, *small, dma, dma((2,)), *exchange_sems],
+                out_specs=[vmem] * 4,
+                scratch_shapes=[
+                    wide,
+                    gathered,
+                    pltpu.VMEM((queue, half), jnp.bfloat16),
+                    pltpu.VMEM((queue, HEAD_WIDTH), jnp.float32),
+                    pltpu.VMEM((2, rows, half), jnp.float32),
+                    *small,
+                    dma,
+                    dma((2,)),
+                    *exchange_sems,
+                ],
                 compiler_params=talk,
             )(keys, values, queries, prompt_length, span_order)
             return pl.pallas_call(
-                functools.partial(mix_kernel, group),
+                functools.partial(mix_kernel, cols_x, group),
                 out_shape=out_shape,
-                in_specs=[vmem] * 3,
+                in_specs=[vmem] * 4,
                 out_specs=hbm,
                 scratch_shapes=[wide, out_sems],
                 compiler_params=quiet,
@@ -444,7 +495,7 @@
             compiler_params=talk,
         )(keys, values)
         return pl.pallas_call(
-            functools.partial(attend_kernel, group, spans),
+            functools.partial(attend_kernel, rows_z, cols_x, group, spans),
             out_shape=out_shape,
             in_specs=[hbm, vmem, vmem, hbm, hbm],
             out_specs=hbm,

time: 15.5 us -> 15.3 us (0.987)
  Pallas kernels: 14.7 us -> 14.4 us
    pallas_call x2, Pallas kernels: 14.7 us -> 14.4 us  [the longest x1 13.3 us: shards(): pl.pallas_call(functools.partial(pair_kernel, rows_z, cols_x, group, span...]
where the time goes in v3:
time: 15.3 us; the launch traced here: 15.1 us
  Pallas kernels  14.4 us (94%)
  between operations  0.66 us (4%)
    pallas_call x1, Pallas kernels, shards(): pl.pallas_call(functools.partial(pair_kernel, rows_z, cols_x, group, span...  13.3 us
    pallas_call x1, Pallas kernels, shards(): pl.pallas_call(functools.partial(mix_kernel, cols_x, group), out_shape=ou...  1.16 us

profile of v3, /device:TPU:12, one launch (start us, length us, event | category | flops | bytes accessed | tf_op | source)
XLA Modules:
  0.0 15.1 jit_solution(3095909639482423412)
XLA Ops:
  0.7 13.3 %shard_map.55 = (bf16[2048,256]{1,0:T(8,128)(2,1)S(1)}, bf16[512,256]{1,0:T(8,128)(2,1)S(1)}, f32[2048,256]{1,0:T(8,128)S(1)}, f32[64,128]{1,0:T(8,128)S(1)}) custom-call(bf16[1,64,256]{2,1,0:T(8,128)(2,1)} %k_hbm.1, bf16[1,64,256]{2,1,0:T(8,128)(2,1)} %v_hbm.1, bf16[1,64,4096]{2,1,0:T(8,128)(2,1)} %q_hbm.1, s32[1]{0:T(128)S(6)} %copy.6.len_hbm, s32[16]{0:T(128)} %order_hbm.1), custom_call_target="tpu_custom_call" | custom-call | tf_op jit(solution)/shard_map/pallas_call | solution.py:458
  13.9 1.2 %shard_map.56 = bf16[1,64,4096]{2,1,0:T(8,128)(2,1)} custom-call(bf16[2048,256]{1,0:T(8,128)(2,1)S(1)} %get-tuple-element.9.w_ref, bf16[512,256]{1,0:T(8,128)(2,1)S(1)} %get-tuple-element.10.v_ref, f32[2048,256]{1,0:T(8,128)S(1)} %get-tuple-element.11.acc_ref, f32[64,128]{1,0:T(8,128)S(1)} %get-tuple-element.12.live_ref), custom_call_target="tpu_custom_call" | custom-call | tf_op jit(solution)/shard_map/pallas_call | solution.py:481

commit v4 on v3

--- a/solution.py
+++ b/solution.py
@@ -52,6 +52,7 @@
     me = lax.axis_index("blk")
     z, x = lax.div(me, cols_x), lax.rem(me, cols_x)
     even = lax.rem(z, 2) == 0
+    first = lax.axis_index("head") == 0
     near = range(1, rows_z)
     far = range(rows_z - 1, 0, -1)
     own = pl.ds((x * rows_z + z) * rows, rows)
@@ -107,23 +108,26 @@
         below(d, lambda row: signal(ready_z.at[z], row, x))
     left(lambda col: signal(ready_x.at[x], z, col))
 
-    def direct(d, visit):
-        if d == 2:
-            pl.when(even)(visit)
-        else:
-            visit()
+    def straight(u):
+        return first & (u == 1)
 
     def send_below(u):
         for d in far:
-            direct(d, lambda d=d: below(d, lambda row: z_copy(z, row, u, sources[u].at[0]).start()))
+            go = functools.partial(below, d, lambda row: z_copy(z, row, u, sources[u].at[0]).start())
+            if d == 2:
+                pl.when(even | straight(u))(go)
+            else:
+                go()
 
     def send_above(d, *which):
-        def go(row):
-            for u in which:
-                z_copy(z, row, u, sources[u].at[0]).start()
-
-        if d != 3:
-            direct(d, lambda: above(d, go))
+        for u in which:
+            go = functools.partial(above, d, lambda row, u=u: z_copy(z, row, u, sources[u].at[0]).start())
+            if d == 2:
+                pl.when(even)(go)
+            elif d == 3:
+                pl.when(straight(u))(go)
+            else:
+                go()
 
     def answered(d):
         above(d, lambda row: pl.semaphore_wait(ready_z.at[row], 1))
@@ -134,7 +138,7 @@
             if d == 1:
                 pl.when(even & (z + 1 < rows_z))(lambda: z_copy(row, z + 1, u).start())
             if d == 2:
-                above(1, lambda to_row: z_copy(row, to_row, u).start())
+                pl.when((z + 1 < rows_z) & ~straight(u))(lambda: z_copy(row, z + 1, u).start())
             spread(row, u)
 
         below(d, take)
@@ -144,7 +148,7 @@
             z_copy(row, z, u).wait_recv()
             spread(row, u)
             if d == 1:
-                pl.when(even & (z >= 1))(lambda: z_copy(row, z - 1, u).start())
+                pl.when(even & (z >= 1) & ~straight(u))(lambda: z_copy(row, z - 1, u).start())
 
         above(d, take)
 
@@ -179,11 +183,11 @@
             answered(d)
             send_above(d, 0)
 
-    first = lax.axis_index("head") == 0
     pl.when(first)(eager)
     pl.when(~first)(patient)
     prepare()
     lowest = first & (z == 0)
+    inner = first & (z > 0) & (z < rows_z - 1)
 
     def values_now():
         send_below(1)
@@ -194,13 +198,14 @@
         relay(d, 0)
         if d == 1:
             pl.when(lowest)(lambda: relay_from_above(1, 1))
+            pl.when(inner)(lambda: relay_from_below(1, 1))
             pl.when(~first)(values_now)
-    for d in near:
+    pl.when(~inner)(lambda: relay_from_below(1, 1))
+    for d in near[1:]:
         relay_from_below(d, 1)
-        if d == 1:
-            pl.when(~lowest)(lambda: relay_from_above(1, 1))
-        else:
-            relay_from_above(d, 1)
+    pl.when(~lowest)(lambda: relay_from_above(1, 1))
+    for d in near[1:]:
+        relay_from_above(d, 1)
     own_keys()
 
     def many(u, count, sem):
@@ -212,19 +217,22 @@
     def arrived(u):
         many(u, along_x, x_recv.at[u]).wait()
 
-    def sent_along_z(row):
-        count = rows_z - 1 - (row + 3 < rows_z)
-        if row % 2 == 1:
-            count -= (row >= 2) + (row + 2 < rows_z)
-        elif 0 < row < rows_z - 1:
-            count += 2
-        return count + (row >= 2 and row + 1 < rows_z)
+    def sent_along_z(row, detours):
+        odd, inside = row % 2 == 1, 0 < row < rows_z - 1
+        count = rows_z - 1 - (odd and row + 2 < rows_z) + (not odd and inside)
+        if detours:
+            count += (row >= 2 and row + 1 < rows_z) - (row + 3 < rows_z)
+            count += (not odd and inside) - (odd and row >= 2)
+        return count
 
     def drain():
         for u in range(2):
             many(u, along_x, x_send.at[u]).wait()
             for row in range(rows_z):
-                pl.when(z == row)(lambda row=row: many(u, sent_along_z(row), z_send.at[u]).wait())
+                for detours in (True, False):
+                    here = (z == row) & (straight(u) != detours)
+                    count = sent_along_z(row, detours)
+                    pl.when(here)(lambda u=u, count=count: many(u, count, z_send.at[u]).wait())
 
     return arrived, drain
 

time: 15.3 us -> 15.1 us (0.987)
  Pallas kernels: 14.4 us -> 14.2 us
    pallas_call x1, Pallas kernels: 13.3 us -> 13 us  [shards(): pl.pallas_call(functools.partial(pair_kernel, rows_z, cols_x, group, span...]
where the time goes in v4:
time: 15.1 us; the launch traced here: 14.9 us
  Pallas kernels  14.2 us (94%)
  between operations  0.66 us (4%)
    pallas_call x1, Pallas kernels, shards(): pl.pallas_call(functools.partial(pair_kernel, rows_z, cols_x, group, span...  13 us
    pallas_call x1, Pallas kernels, shards(): pl.pallas_call(functools.partial(mix_kernel, cols_x, group), out_shape=ou...  1.16 us

profile of v4, /device:TPU:12, one launch (start us, length us, event | category | flops | bytes accessed | tf_op | source)
XLA Modules:
  0.0 14.9 jit_solution(11083842621207473334)
XLA Ops:
  0.7 13.0 %shard_map.55 = (bf16[2048,256]{1,0:T(8,128)(2,1)S(1)}, bf16[512,256]{1,0:T(8,128)(2,1)S(1)}, f32[2048,256]{1,0:T(8,128)S(1)}, f32[64,128]{1,0:T(8,128)S(1)}) custom-call(bf16[1,64,256]{2,1,0:T(8,128)(2,1)} %k_hbm.1, bf16[1,64,256]{2,1,0:T(8,128)(2,1)} %v_hbm.1, bf16[1,64,4096]{2,1,0:T(8,128)(2,1)} %q_hbm.1, s32[1]{0:T(128)S(6)} %copy.6.len_hbm, s32[16]{0:T(128)} %order_hbm.1), custom_call_target="tpu_custom_call" | custom-call | tf_op jit(solution)/shard_map/pallas_call | solution.py:466
  13.7 1.2 %shard_map.56 = bf16[1,64,4096]{2,1,0:T(8,128)(2,1)} custom-call(bf16[2048,256]{1,0:T(8,128)(2,1)S(1)} %get-tuple-element.9.w_ref, bf16[512,256]{1,0:T(8,128)(2,1)S(1)} %get-tuple-element.10.v_ref, f32[2048,256]{1,0:T(8,128)S(1)} %get-tuple-element.11.acc_ref, f32[64,128]{1,0:T(8,128)S(1)} %get-tuple-element.12.live_ref), custom_call_target="tpu_custom_call" | custom-call | tf_op jit(solution)/shard_map/pallas_call | solution.py:489

commit v5 on v4

--- a/solution.py
+++ b/solution.py
@@ -187,7 +187,7 @@
     pl.when(~first)(patient)
     prepare()
     lowest = first & (z == 0)
-    inner = first & (z > 0) & (z < rows_z - 1)
+    upper = first & (z > 0)
 
     def values_now():
         send_below(1)
@@ -198,9 +198,9 @@
         relay(d, 0)
         if d == 1:
             pl.when(lowest)(lambda: relay_from_above(1, 1))
-            pl.when(inner)(lambda: relay_from_below(1, 1))
+            pl.when(upper)(lambda: relay_from_below(1, 1))
             pl.when(~first)(values_now)
-    pl.when(~inner)(lambda: relay_from_below(1, 1))
+    pl.when(~upper)(lambda: relay_from_below(1, 1))
     for d in near[1:]:
         relay_from_below(d, 1)
     pl.when(~lowest)(lambda: relay_from_above(1, 1))

time: 15.1 us -> 15 us (level)
  no operation moved by 1% of the time
where the time goes in v5:
time: 15 us; the launch traced here: 14.9 us
  Pallas kernels  14.2 us (95%)
  between operations  0.66 us (4%)
    pallas_call x1, Pallas kernels, shards(): pl.pallas_call(functools.partial(pair_kernel, rows_z, cols_x, group, span...  13 us
    pallas_call x1, Pallas kernels, shards(): pl.pallas_call(functools.partial(mix_kernel, cols_x, group), out_shape=ou...  1.16 us

profile of v5, /device:TPU:12, one launch (start us, length us, event | category | flops | bytes accessed | tf_op | source)
XLA Modules:
  0.0 14.9 jit_solution(17860034164424395132)
XLA Ops:
  0.7 13.0 %shard_map.55 = (bf16[2048,256]{1,0:T(8,128)(2,1)S(1)}, bf16[512,256]{1,0:T(8,128)(2,1)S(1)}, f32[2048,256]{1,0:T(8,128)S(1)}, f32[64,128]{1,0:T(8,128)S(1)}) custom-call(bf16[1,64,256]{2,1,0:T(8,128)(2,1)} %k_hbm.1, bf16[1,64,256]{2,1,0:T(8,128)(2,1)} %v_hbm.1, bf16[1,64,4096]{2,1,0:T(8,128)(2,1)} %q_hbm.1, s32[1]{0:T(128)S(6)} %copy.6.len_hbm, s32[16]{0:T(128)} %order_hbm.1), custom_call_target="tpu_custom_call" | custom-call | tf_op jit(solution)/shard_map/pallas_call | solution.py:466
  13.7 1.2 %shard_map.56 = bf16[1,64,4096]{2,1,0:T(8,128)(2,1)} custom-call(bf16[2048,256]{1,0:T(8,128)(2,1)S(1)} %get-tuple-element.9.w_ref, bf16[512,256]{1,0:T(8,128)(2,1)S(1)} %get-tuple-element.10.v_ref, f32[2048,256]{1,0:T(8,128)S(1)} %get-tuple-element.11.acc_ref, f32[64,128]{1,0:T(8,128)S(1)} %get-tuple-element.12.live_ref), custom_call_target="tpu_custom_call" | custom-call | tf_op jit(solution)/shard_map/pallas_call | solution.py:489

commit v6 on v5

--- a/solution.py
+++ b/solution.py
@@ -12,7 +12,7 @@
 NEG_FILL = -1e30
 HEADS_PER_TILE = 2
 KEY_CHUNK = 512
-OUT_PARTS = 2
+OUT_PARTS = 1
 VMEM_LIMIT = 40 * 1024 * 1024
 MESH = pl.DeviceIdType.MESH
 
@@ -73,7 +73,7 @@
         )
 
     def z_copy(row, to_row, u, source=None):
-        return send(source, u, row, to_row, x, z_send.at[u], z_recv.at[row, u])
+        return send(source, u, row, to_row, x, z_send.at[u], z_recv.at[row - jnp.where(row > to_row, 1, 0), u])
 
     def x_copy(row, col, u):
         return send(None, u, row, z, col, x_send.at[u], x_recv.at[u])
@@ -105,8 +105,8 @@
     right(lambda col: signal(barrier, z, col))
     pl.when(z + x > 0)(lambda: pl.semaphore_wait(barrier, z + x))
     for d in far:
-        below(d, lambda row: signal(ready_z.at[z], row, x))
-    left(lambda col: signal(ready_x.at[x], z, col))
+        below(d, lambda row: signal(ready_z.at[z - 1], row, x))
+    left(lambda col: signal(ready_x.at[x - 1], z, col))
 
     def straight(u):
         return first & (u == 1)
@@ -130,7 +130,7 @@
                 go()
 
     def answered(d):
-        above(d, lambda row: pl.semaphore_wait(ready_z.at[row], 1))
+        above(d, lambda row: pl.semaphore_wait(ready_z.at[row - 1], 1))
 
     def relay_from_below(d, u):
         def take(row):
@@ -161,7 +161,7 @@
         left(lambda col: x_copy(z, col, u).start())
 
     def send_right(*which):
-        right(lambda col: pl.semaphore_wait(ready_x.at[col], 1))
+        right(lambda col: pl.semaphore_wait(ready_x.at[col - 1], 1))
         for u in which:
             right(lambda col: x_copy(z, col, u).start())
 
@@ -445,11 +445,11 @@
         )
         exchange_sems = [
             dma((2,)),
-            pltpu.SemaphoreType.REGULAR((rows_z,)),
-            pltpu.SemaphoreType.REGULAR((cols_x,)),
+            pltpu.SemaphoreType.REGULAR((max(rows_z - 1, 1),)),
+            pltpu.SemaphoreType.REGULAR((max(cols_x - 1, 1),)),
             dma((2,)),
             dma((2,)),
-            dma((rows_z, 2)),
+            dma((max(rows_z - 1, 1), 2)),
             dma((2,)),
         ]
         small = [pltpu.SMEM(prompt_length.shape, jnp.int32), pltpu.SMEM(span_order.shape, jnp.int32)]

time: 15 us -> 15 us (level)
  no operation moved by 1% of the time
where the time goes in v6:
time: 15 us; the launch traced here: 14.9 us
  Pallas kernels  14.2 us (95%)
  between operations  0.66 us (4%)
    pallas_call x1, Pallas kernels, shards(): pl.pallas_call(functools.partial(pair_kernel, rows_z, cols_x, group, span...  13 us
    pallas_call x1, Pallas kernels, shards(): pl.pallas_call(functools.partial(mix_kernel, cols_x, group), out_shape=ou...  1.19 us

profile of v6, /device:TPU:12, one launch (start us, length us, event | category | flops | bytes accessed | tf_op | source)
XLA Modules:
  0.0 14.9 jit_solution(6244538933146397035)
XLA Ops:
  0.7 13.0 %shard_map.55 = (bf16[2048,256]{1,0:T(8,128)(2,1)S(1)}, bf16[512,256]{1,0:T(8,128)(2,1)S(1)}, f32[2048,256]{1,0:T(8,128)S(1)}, f32[64,128]{1,0:T(8,128)S(1)}) custom-call(bf16[1,64,256]{2,1,0:T(8,128)(2,1)} %k_hbm.1, bf16[1,64,256]{2,1,0:T(8,128)(2,1)} %v_hbm.1, bf16[1,64,4096]{2,1,0:T(8,128)(2,1)} %q_hbm.1, s32[1]{0:T(128)S(6)} %copy.6.len_hbm, s32[16]{0:T(128)} %order_hbm.1), custom_call_target="tpu_custom_call" | custom-call | tf_op jit(solution)/shard_map/pallas_call | solution.py:466
  13.7 1.2 %shard_map.56 = bf16[1,64,4096]{2,1,0:T(8,128)(2,1)} custom-call(bf16[2048,256]{1,0:T(8,128)(2,1)S(1)} %get-tuple-element.9.w_ref, bf16[512,256]{1,0:T(8,128)(2,1)S(1)} %get-tuple-element.10.v_ref, f32[2048,256]{1,0:T(8,128)S(1)} %get-tuple-element.11.acc_ref, f32[64,128]{1,0:T(8,128)S(1)} %get-tuple-element.12.live_ref), custom_call_target="tpu_custom_call" | custom-call | tf_op jit(solution)/shard_map/pallas_call | solution.py:489
